TPU v7x, 128 devices: a whole 4x4x4 slice. The times are simulated.
128 devices in a mesh: row: 16 (over z, x), col: 8 (over y, core).
Axes of the slice: x: 4, y: 4, z: 4, core: 2. Of those that a mesh axis runs over, the one named last changes fastest.
Arguments:
- tokens: bfloat16 [1024, 12288], P('col', 'row'), may hold values from -16 to 16
- norm_gain: float32 [12288], P('row'), may hold values from 0.25 to 1.75
- weight_in: bfloat16 [12288, 49152], P('row', 'col'), may hold values from -0.0546875 to 0.0546875
- weight_out: bfloat16 [49152, 12288], P('col', 'row'), may hold values from -0.02734375 to 0.02734375
Outputs:
- mixed: bfloat16 [1024, 12288], P('col', 'row')
All inputs are finite; a program needn't handle non-finite values.
Results may differ from a plain program's by a relative error of at most 0.0051.
Values may be sent and summed in bfloat16 or wider, within the bound.
A program may use at most 128 MiB of HBM per device.

v0:
```python
import jax
import jax.numpy as jnp
from jax import lax
from jax.sharding import PartitionSpec as P

D = 12288


epsilon = 1e-05


def per_device(tokens, norm_gain, weight_in, weight_out):
    gathered = lax.all_gather(tokens, "col", axis=0, tiled=True)
    wide_input = gathered.astype(jnp.float32)
    scaled = (wide_input * norm_gain[None, :]).astype(jnp.bfloat16)
    squares = jnp.sum(wide_input * wide_input, axis=1)
    token_total = gathered.shape[0]
    row_count = token_total // lax.axis_size("row")
    square_all = lax.psum(squares, "row")
    inverse_all = lax.rsqrt(square_all / D + epsilon)
    hidden_sum = lax.psum_scatter(
        jnp.dot(scaled, weight_in, preferred_element_type=jnp.float32),
        "row",
        scatter_dimension=0,
        tiled=True,
    )
    inverse = lax.dynamic_slice_in_dim(inverse_all, lax.axis_index("row") * row_count, row_count, 0)
    hidden = hidden_sum * inverse[:, None]
    active = jax.nn.gelu(hidden, approximate=True).astype(jnp.bfloat16)
    branch = jnp.dot(
        lax.all_gather(active, "row", axis=0, tiled=True),
        weight_out,
        preferred_element_type=jnp.float32,
    )
    output_rows = lax.psum_scatter(branch, "col", scatter_dimension=0, tiled=True)
    return (tokens.astype(jnp.float32) + output_rows).astype(jnp.bfloat16)


def solution(mesh):
    in_specs = (P("col", "row"), P("row"), P("row", "col"), P("col", "row"))
    out_specs = P("col", "row")
    return jax.shard_map(
        per_device, mesh=mesh, in_specs=in_specs, out_specs=out_specs, check_vma=False
    )
```

profile of v0, /device:TPU:1, one launch (start us, length us, event | category | flops | bytes accessed | tf_op | source)
XLA Modules:
  0.0 357.5 jit_solution(11592695084648241998)
XLA Ops:
  6.5 0.0 all-gather.3.cloned.1.call-start
  6.5 0.7 all-gather.3.cloned.1.call-update
  7.3 0.0 reduce-scatter.3.cloned.1.call-start
  7.3 29.6 %all-gather.3.cloned.1.call-done = bf16[1024,768]{1,0:T(8,128)(2,1)} async-done(((bf16[128,768]{1,0:T(8,128)(2,1)}), bf16[1024,768]{1,0:T(8,128)(2,1)}) %all-gather.3.cloned.1.call-update) | async-done | bytes 1572880 | tf_op jit(solution)/shard_map/all_gather | solution.py:13
  36.9 17.6 %fusion.10 = f32[1024,6144]{1,0:T(8,128)} fusion(bf16[768,6144]{1,0:T(8,128)(2,1)} %param.6, bf16[1024,768]{1,0:T(8,128)(2,1)} %all-gather.3.cloned.1.call-done, f32[768]{0:T(1024)} %param.5), kind=kOutput, calls=%fused_computation.13 | convolution fusion | flops 9666035712 | bytes 36178944 | tf_op jit(solution)/shard_map/dot_general | solution.py:22
  54.5 0.0 copy-start
  54.5 0.0 reduce-scatter.3.cloned.1.call-update
  54.5 0.0 all-gather.5.cloned.1.call-start
  54.6 1.3 copy-done
  55.9 0.4 fusion.1
  56.3 34.8 %psum.7 = f32[1024]{0:T(1024)S(1)} all-reduce(f32[1024]{0:T(1024)S(1)} %fusion.1), channel_id=1, replica_groups=mesh['row'=16,'col'=8] {'row'}, use_global_device_ids=true, to_apply=%region_2.0 | all-reduce | flops 1024 | bytes 8192 | tf_op jit(solution)/shard_map/psum | solution.py:19
  91.0 0.1 dynamic_slice.3
  91.1 116.9 %reduce-scatter.3.cloned.1.call-done = f32[64,6144]{1,0:T(8,128)} async-done(((f32[1024,6144]{1,0:T(8,128)}), f32[64,6144]{1,0:T(8,128)}) %reduce-scatter.3.cloned.1.call-update) | async-done | bytes 1572880 | tf_op jit(solution)/shard_map/reduce_scatter | solution.py:21
  208.0 2.9 fusion.9
  210.9 0.0 all-gather.5.cloned.1.call-update
  210.9 0.0 reduce-scatter.5.cloned.1.call-start
  211.0 89.5 %all-gather.5.cloned.1.call-done = bf16[1024,6144]{1,0:T(8,128)(2,1)} async-done(((bf16[64,6144]{1,0:T(8,128)(2,1)}), bf16[1024,6144]{1,0:T(8,128)(2,1)}) %all-gather.5.cloned.1.call-update) | async-done | bytes 12582928 | tf_op jit(solution)/shard_map/all_gather | solution.py:31
  300.5 15.9 %fusion.13 = f32[1024,768]{1,0:T(8,128)} fusion(bf16[1024,6144]{1,0:T(8,128)(2,1)} %all-gather.5.cloned.1.call-done, bf16[6144,768]{1,0:T(8,128)(2,1)} %param.7), kind=kOutput, calls=%fused_computation.17 | convolution fusion | flops 9663676416 | bytes 25165824 | tf_op jit(solution)/shard_map/dot_general | solution.py:30
  316.4 0.0 copy-start.1
  316.4 0.0 reduce-scatter.5.cloned.1.call-update
  316.4 32.9 %reduce-scatter.5.cloned.1.call-done = f32[128,768]{1,0:T(8,128)} async-done(((f32[1024,768]{1,0:T(8,128)}), f32[128,768]{1,0:T(8,128)}) %reduce-scatter.5.cloned.1.call-update) | async-done | bytes 393232 | tf_op jit(solution)/shard_map/reduce_scatter | solution.py:35
  349.3 0.0 copy-done.1
  349.3 1.7 add_convert_fusion
  (1 shorter events, 0.0 us)
Async XLA Ops:
  6.5 30.4 %all-gather.3.cloned.1.call-start = ((), (), s32[]{:S(2)}) async-start(), calls=%async_computation.2 | async-start | bytes 1769472 | tf_op jit(solution)/shard_map/all_gather | solution.py:13
  7.3 200.7 %reduce-scatter.3.cloned.1.call-start = ((), (), s32[]{:S(2)}) async-start(), calls=%async_computation.3 | async-start | bytes 26738688 | tf_op jit(solution)/shard_map/reduce_scatter | solution.py:21
  54.5 1.4 copy-start
  54.5 245.9 %all-gather.5.cloned.1.call-start = ((), (), s32[]{:S(2)}) async-start(), calls=%async_computation.4 | async-start | bytes 13369344 | tf_op jit(solution)/shard_map/all_gather | solution.py:31
  210.9 138.4 %reduce-scatter.5.cloned.1.call-start = ((), (), s32[]{:S(2)}) async-start(), calls=%async_computation.5 | async-start | bytes 3538944 | tf_op jit(solution)/shard_map/reduce_scatter | solution.py:35
  316.4 32.9 %copy-start.1 = (bf16[128,768]{1,0:T(8,128)(2,1)S(1)}, bf16[128,768]{1,0:T(8,128)(2,1)}, u32[]{:S(2)}) copy-start(bf16[128,768]{1,0:T(8,128)(2,1)} %param.4) | copy-start | bytes 589828
Sparse Core Ops, SparseCore 0:
  9.0 27.8 all-gather.2
  54.6 153.2 reduce-scatter.2
  211.0 89.3 all-gather.4
  316.5 32.6 reduce-scatter.4
where the time goes:
time: 360 us; the launch traced here: 358 us
  waiting for transfers between devices  270 us (75%)
  blocking collectives  34.8 us (10%)
  matrix products  33.5 us (9%)
  between operations  13.1 us (4%)
  other arithmetic  5.03 us (1%)
    reduce_scatter x1, waiting for transfers between devices, per_device(): lax.psum_scatter(jnp.dot(scaled, weight_in, preferred_element_type=jnp.fl...  117 us
    all_gather x1, waiting for transfers between devices, per_device(): lax.all_gather(active, 'row', axis=0, tiled=True)  89.5 us
    psum x1, blocking collectives, per_device(): square_all = lax.psum(squares, 'row')  34.8 us
    reduce_scatter x1, waiting for transfers between devices, per_device(): lax.psum_scatter(branch, 'col', scatter_dimension=0, tiled=True)  32.9 us
    all_gather x1, waiting for transfers between devices, per_device(): gathered = lax.all_gather(tokens, 'col', axis=0, tiled=True)  29.6 us
    dot_general x1, matrix products, per_device(): jnp.dot(scaled, weight_in, preferred_element_type=jnp.float32)  17.6 us
    dot_general x1, matrix products, per_device(): jnp.dot(lax.all_gather(active, 'row', axis=0, tiled=True), weight_out, pr...  15.9 us
  transfers between devices with their start and end apart: 4, of which 4 were waited for; matrix products, arithmetic and copies ran while one was open for 0% of the time, Pallas kernels for 0%

commit v1 on v0

v1 whole, which is shorter than its diff:
```python
import functools

import jax
import jax.numpy as jnp
from jax import lax
from jax.experimental import pallas as pl
from jax.experimental.pallas import tpu as pltpu
from jax.sharding import PartitionSpec as P

D = 12288
EPSILON = 1e-05
MESH = pl.DeviceIdType.MESH
F32, BF16 = jnp.float32, jnp.bfloat16

WAVES = 4
LANES = 8
NARROW = 768
BLOCK = 16
TILE = 256


def gelu(v):
    return 0.5 * v * (1.0 + jnp.tanh(0.7978845608028654 * (v + 0.044715 * (v * v * v))))


def kernel(
    tokens_ref, gain_ref, w1_hbm, w2_hbm, out_ref,
    w1, w2, raw, scaled, rs1, rs2, total, active, branch, own, out_send, out_recv, squares, inverse,
    w1_sem, w2_sem, tok_ssem, tok_rsem, out_ssem, out_rsem, sq_ssem, sq_rsem, ring_ssem, ring_rsem,
):
    row, col = lax.axis_index("row"), lax.axis_index("col")
    x, z = lax.rem(row, 4), lax.div(row, 4)

    def w1_copy(s):
        return pltpu.make_async_copy(w1_hbm.at[:, pl.ds(pl.multiple_of(s * NARROW, NARROW), NARROW)], w1.at[s], w1_sem.at[s])

    def w2_copy(s):
        return pltpu.make_async_copy(w2_hbm.at[pl.ds(pl.multiple_of(s * NARROW, NARROW), NARROW)], w2.at[s], w2_sem.at[s])

    for s in range(LANES):
        w1_copy(s).start()
    for s in range(LANES):
        w2_copy(s).start()

    barrier = pltpu.get_barrier_semaphore()
    for i in range(1, 8):
        pl.semaphore_signal(barrier, inc=1, device_id=(row, lax.rem(col + i, 8)), device_id_type=MESH)
    for i in range(1, 16):
        pl.semaphore_signal(barrier, inc=1, device_id=(lax.rem(row + i, 16), col), device_id_type=MESH)
    pl.semaphore_wait(barrier, 22)

    def tok_copy(w, i):
        return pltpu.make_async_remote_copy(
            src_ref=tokens_ref.at[w], dst_ref=raw.at[col, w],
            send_sem=tok_ssem.at[w, i], recv_sem=tok_rsem.at[w, i],
            device_id=(row, lax.rem(col + i, 8)), device_id_type=MESH,
        )

    for w in range(WAVES):
        for i in range(1, 8):
            tok_copy(w, i).start()
    raw[col] = tokens_ref[...]

    def place(s):
        second = lax.rem(s, 2)
        step = 1 - 2 * lax.rem(lax.div(s, 2), 2)
        p = x * (1 - second) + z * second
        q = z * (1 - second) + x * second
        p_next, q_next = lax.rem(p + step + 4, 4), lax.rem(q + step + 4, 4)
        first_row = second * (p_next * 4 + q) + (1 - second) * (q * 4 + p_next)
        second_row = second * (p * 4 + q_next) + (1 - second) * (q_next * 4 + p)
        return p, q, step, first_row, second_row

    def ring_copy(kind, w, s, k, src, dst, target):
        return pltpu.make_async_remote_copy(
            src_ref=src, dst_ref=dst,
            send_sem=ring_ssem.at[kind, s, k], recv_sem=ring_rsem.at[kind, w, s, k],
            device_id=(target, col), device_id_type=MESH,
        )

    def around(v):
        return lax.rem(v + 8, 4)

    def rs1_copy(w, s, k, target):
        return ring_copy(0, w, s, k, rs1.at[w, s, (k + 3) % 4], rs1.at[w, s, k], target)

    def rs2_copy(w, s, k, target):
        return ring_copy(1, w, s, k, rs2.at[w, s, (k + 3) % 4], rs2.at[w, s, k], target)

    def ag2_copy(w, s, k, p, q, step, target):
        block = active.at[w, s, p * 4 + around(q - step * k)]
        return ring_copy(2, w, s, k, block, block, target)

    def ag1_copy(w, s, k, p, step, target):
        chunk = active.at[w, s, pl.ds(around(p - step * k) * 4, 4)]
        return ring_copy(3, w, s, k, chunk, chunk, target)

    def product(w, s, j, t):
        a = scaled[w, pl.ds(j * 4, 4)].reshape(64, NARROW)
        return jnp.dot(a, w1[s, :, t * TILE:(t + 1) * TILE], preferred_element_type=F32).reshape(4, BLOCK, TILE)

    def rs1_event(w, s, k):
        p, q, step, target, _ = place(s)
        j = around(p - step * (k + 1))
        slot = (k + 3) % 4
        if k > 0:
            rs1_copy(w, s, k - 1, target).wait_recv()
        for t in range(NARROW // TILE):
            part = product(w, s, j, t)
            if k > 0:
                part = part + rs1[w, s, slot, :, :, t * TILE:(t + 1) * TILE].astype(F32)
            rs1[w, s, slot, :, :, t * TILE:(t + 1) * TILE] = part.astype(BF16)

        @pl.when(w > 0)
        def _():
            rs1_copy(w, s, k, target).wait_send()

        rs1_copy(w, s, k, target).start()

    def rs2_event(w, s, k):
        p, q, step, before, target = place(s)
        j = around(q - step * (k + 1))
        slot = (k + 3) % 4
        if k == 0:
            rs1_copy(w, s, 2, before).wait_recv()
            for t in range(NARROW // TILE):
                cols = slice(t * TILE, (t + 1) * TILE)
                total[s, :, :, cols] = product(w, s, p, t) + rs1[w, s, 2, :, :, cols].astype(F32)
            rs2[w, s, slot] = total[s, j].astype(BF16)
        else:
            rs2_copy(w, s, k - 1, target).wait_recv()
            rs2[w, s, slot] = (rs2[w, s, slot].astype(F32) + total[s, j]).astype(BF16)

        @pl.when(w > 0)
        def _():
            rs2_copy(w, s, k, target).wait_send()

        rs2_copy(w, s, k, target).start()

    def ag2_event(w, s, k):
        p, q, step, _, target = place(s)
        if k == 0:
            rs2_copy(w, s, 2, target).wait_recv()
            b = p * 4 + q
            c, first = lax.div(b, 2), 32 * w + 16 * lax.rem(b, 2)
            sub = lax.broadcasted_iota(jnp.int32, (8, 128), 0)
            line = jnp.sum(jnp.where(sub == c, inverse[...], 0.0), axis=0, keepdims=True)
            spot = lax.broadcasted_iota(jnp.int32, (BLOCK, 128), 1) == lax.broadcasted_iota(jnp.int32, (BLOCK, 128), 0) + first
            scale = jnp.sum(jnp.where(spot, jnp.broadcast_to(line, (BLOCK, 128)), 0.0), axis=1, keepdims=True)
            hidden = (rs2[w, s, 2].astype(F32) + total[s, q]) * scale
            active[w, s, b] = gelu(hidden).astype(BF16)
        else:
            ag2_copy(w, s, k - 1, p, q, step, target).wait_recv()

        @pl.when(w > 0)
        def _():
            ag2_copy(w, s, k, p, q, step, target).wait_send()

        ag2_copy(w, s, k, p, q, step, target).start()

    def ag1_event(w, s, k):
        p, q, step, target, before = place(s)
        if k == 0:
            ag2_copy(w, s, 2, p, q, step, before).wait_recv()
        else:
            ag1_copy(w, s, k - 1, p, step, target).wait_recv()

        @pl.when(w > 0)
        def _():
            ag1_copy(w, s, k, p, step, target).wait_send()

        ag1_copy(w, s, k, p, step, target).start()

    def out_copy(w, i):
        peer = lax.rem(col + i, 8)
        return pltpu.make_async_remote_copy(
            src_ref=out_send.at[w, peer], dst_ref=out_recv.at[w, col],
            send_sem=out_ssem.at[w, i], recv_sem=out_rsem.at[w, i],
            device_id=(row, peer), device_id_type=MESH,
        )

    def finish(w, s):
        p, q, step, target, _ = place(s)
        ag1_copy(w, s, 2, p, step, target).wait_recv()

        @pl.when(w == 0)
        def _():
            w2_copy(s).wait()

        def tile(t, carry):
            cols = pl.ds(pl.multiple_of(t * TILE, TILE), TILE)
            got = jnp.dot(active[w, s].reshape(256, NARROW), w2[s, :, cols], preferred_element_type=F32)
            branch[:, cols] = jnp.where(s == 0, 0.0, branch[:, cols]) + got
            return carry

        lax.fori_loop(0, 3, tile, 0)

        @pl.when(s == LANES - 1)
        def _():
            out_send[w] = branch[...].reshape(8, 32, NARROW).astype(BF16)
            own[w] = branch[pl.ds(pl.multiple_of(col * 32, 32), 32)]
            for i in range(1, 8):
                out_copy(w, i).start()

    def deliver(w):
        rows = own[w] + tokens_ref[w].astype(F32)
        for i in range(1, 8):
            out_copy(w, i).wait_recv()
            rows = rows + out_recv[w, lax.rem(col + 8 - i, 8)].astype(F32)
        out_ref[w] = rows.astype(BF16)

    def wait_tokens(w):
        for i in range(1, 8):
            tok_copy(w, i).wait_recv()

    def sq_copy(i):
        return pltpu.make_async_remote_copy(
            src_ref=squares.at[row], dst_ref=squares.at[row],
            send_sem=sq_ssem.at[i], recv_sem=sq_rsem.at[i],
            device_id=(lax.rem(row + i, 16), col), device_id_type=MESH,
        )

    def send_squares():
        ones = jnp.ones((8, NARROW), BF16)
        sub = lax.broadcasted_iota(jnp.int32, (8, 128), 0)

        def one(c, tile):
            v = raw[c].reshape(128, NARROW).astype(F32)
            v = v * v
            high = v.astype(BF16)
            low = (v - high.astype(F32)).astype(BF16)
            dims = (((1,), (1,)), ((), ()))
            sums = lax.dot_general(ones, high, dims, preferred_element_type=F32)
            sums = sums + lax.dot_general(ones, low, dims, preferred_element_type=F32)
            return jnp.where(sub == c, sums, tile)

        squares[row] = lax.fori_loop(0, 8, one, jnp.zeros((8, 128), F32))
        for i in range(1, 16):
            sq_copy(i).start()

    def take_squares():
        for i in range(1, 16):
            sq_copy(i).wait_recv()
        inverse[...] = lax.rsqrt(jnp.sum(squares[...], axis=0) / D + EPSILON)

    def scale_wave(w):
        def one(c, carry):
            v = raw[c, w].astype(F32) * gain_ref[...]
            scaled[w, pl.ds(2 * c, 2)] = v.astype(BF16).reshape(2, BLOCK, NARROW)
            return carry

        lax.fori_loop(0, 8, one, 0)

    def slot(t, carry):
        @pl.when(t == 0)
        def _():
            wait_tokens(0)

        @pl.when(t == 1)
        def _():
            for w in range(1, WAVES):
                wait_tokens(w)

        @pl.when(t < WAVES)
        def _():
            scale_wave(t)

        @pl.when(t == 2)
        def _():
            take_squares()

        for k in range(3):
            def lane(s, carry, k=k):
                if k == 0:
                    @pl.when(t >= 4)
                    def _():
                        finish(t - 4, s)

                    @pl.when(t == 0)
                    def _():
                        w1_copy(s).wait()

                @pl.when((t >= 3) & (t < 7))
                def _():
                    ag1_event(t - 3, s, k)

                @pl.when((t >= 2) & (t < 6))
                def _():
                    ag2_event(t - 2, s, k)

                @pl.when((t >= 1) & (t < 5))
                def _():
                    rs2_event(t - 1, s, k)

                @pl.when(t < 4)
                def _():
                    rs1_event(t, s, k)

                return carry

            lax.fori_loop(0, LANES, lane, 0)

            if k == 0:
                @pl.when(t == 1)
                def _():
                    send_squares()

                @pl.when(t >= 5)
                def _():
                    deliver(t - 5)

        return carry

    lax.fori_loop(0, 7, slot, 0)

    def last(s, carry):
        finish(WAVES - 1, s)
        return carry

    lax.fori_loop(0, LANES, last, 0)
    deliver(WAVES - 2)
    deliver(WAVES - 1)

    def leave(s, carry):
        p, q, step, first_row, second_row = place(s)
        w = WAVES - 1
        for k in range(3):
            rs1_copy(w, s, k, first_row).wait_send()
            rs2_copy(w, s, k, second_row).wait_send()
            ag2_copy(w, s, k, p, q, step, second_row).wait_send()
            ag1_copy(w, s, k, p, step, first_row).wait_send()
        return carry

    lax.fori_loop(0, LANES, leave, 0)
    for i in range(1, 8):
        for w in range(WAVES):
            tok_copy(w, i).wait_send()
            out_copy(w, i).wait_send()
    for i in range(1, 16):
        sq_copy(i).wait_send()


def per_device(tokens, norm_gain, weight_in, weight_out):
    vmem = pl.BlockSpec(memory_space=pltpu.VMEM)
    anywhere = pl.BlockSpec(memory_space=pl.ANY)
    dma = pltpu.SemaphoreType.DMA
    out = pl.pallas_call(
        kernel,
        out_shape=jax.ShapeDtypeStruct((WAVES, 32, NARROW), BF16),
        in_specs=[vmem, vmem, anywhere, anywhere],
        out_specs=vmem,
        scratch_shapes=[
            pltpu.VMEM((LANES, 768, NARROW), BF16),
            pltpu.VMEM((LANES, NARROW, 768), BF16),
            pltpu.VMEM((8, WAVES, 32, 768), BF16),
            pltpu.VMEM((WAVES, 16, BLOCK, 768), BF16),
            pltpu.VMEM((WAVES, LANES, 4, 4, BLOCK, NARROW), BF16),
            pltpu.VMEM((WAVES, LANES, 4, BLOCK, NARROW), BF16),
            pltpu.VMEM((LANES, 4, BLOCK, NARROW), F32),
            pltpu.VMEM((WAVES, LANES, 16, BLOCK, NARROW), BF16),
            pltpu.VMEM((256, 768), F32),
            pltpu.VMEM((WAVES, 32, 768), F32),
            pltpu.VMEM((WAVES, 8, 32, 768), BF16),
            pltpu.VMEM((WAVES, 8, 32, 768), BF16),
            pltpu.VMEM((16, 8, 128), F32),
            pltpu.VMEM((8, 128), F32),
            dma((LANES,)), dma((LANES,)),
            dma((WAVES, 8)), dma((WAVES, 8)),
            dma((WAVES, 8)), dma((WAVES, 8)),
            dma((16,)), dma((16,)),
            dma((4, LANES, 3)), dma((4, WAVES, LANES, 3)),
        ],
        compiler_params=pltpu.CompilerParams(
            collective_id=0, has_side_effects=True, vmem_limit_bytes=67043328
        ),
        name="ffn",
    )(tokens.reshape(WAVES, 32, 768), norm_gain.reshape(1, 768), weight_in, weight_out)
    return out.reshape(128, 768)


def solution(mesh):
    in_specs = (P("col", "row"), P("row"), P("row", "col"), P("col", "row"))
    out_specs = P("col", "row")
    return jax.shard_map(
        per_device, mesh=mesh, in_specs=in_specs, out_specs=out_specs, check_vma=False
    )
```

time: 360 us -> 175 us (0.49)
  waiting for transfers between devices: 270 us -> 0 us
  Pallas kernels: 0 us -> 172 us
  blocking collectives: 34.8 us -> 0 us
  matrix products: 33.5 us -> 0 us
  between operations: 13.1 us -> 0.01 us
  other arithmetic: 5.03 us -> 0 us
    pallas_call x0 -> x1, Pallas kernels: none -> 172 us  [per_device(): pl.pallas_call(kernel, out_shape=jax.ShapeDtypeStruct((WAVES, 32, NARROW)...]
    reduce_scatter x2 -> x0, waiting for transfers between devices: 150 us -> none  [the longest x1 117 us: per_device(): lax.psum_scatter(jnp.dot(scaled, weight_in, preferred_element_type=jnp.fl...]
    all_gather x2 -> x0, waiting for transfers between devices: 119 us -> none  [the longest x1 89.5 us: per_device(): lax.all_gather(active, 'row', axis=0, tiled=True)]
    psum x1 -> x0, blocking collectives: 34.8 us -> none  [per_device(): square_all = lax.psum(squares, 'row')]
    dot_general x2 -> x0, matrix products: 33.5 us -> none  [the longest x1 17.6 us: per_device(): jnp.dot(scaled, weight_in, preferred_element_type=jnp.float32)]
    convert_element_type x2 -> x0, other arithmetic: 4.65 us -> none  [the longest x1 2.94 us: per_device(): active = jax.nn.gelu(hidden, approximate=True).astype(jnp.bfloat16)]
  transfers between devices with their start and end apart: 4 -> 0, of which waited for: 4 -> 0; matrix products, arithmetic and copies ran while one was open for 0% -> 0% of each run, Pallas kernels for 0% -> 0%
where the time goes in v1:
time: 175 us
  Pallas kernels  172 us (98%)
  local copies, waits for them, and re-layouts  2.88 us (2%)
    pallas_call x1, Pallas kernels, per_device(): pl.pallas_call(kernel, out_shape=jax.ShapeDtypeStruct((WAVES, 32, NARROW)...  172 us

profile of v1, /device:TPU:1, one launch (start us, length us, event | category | flops | bytes accessed | tf_op | source)
XLA Modules:
  0.0 174.7 jit_solution(6806052992629270476)
XLA Ops:
  0.0 1.3 reshape.10.gain_ref
  1.3 171.8 %ffn.1 = bf16[4,32,768]{2,1,0:T(8,128)(2,1)} custom-call(bf16[4,32,768]{2,1,0:T(8,128)(2,1)} %bitcast.3, f32[1,768]{1,0:T(1,128)} %reshape.10.gain_ref, bf16[768,6144]{1,0:T(8,128)(2,1)} %w1_hbm.1, bf16[6144,768]{1,0:T(8,128)(2,1)} %w2_hbm.1), custom_call_target="tpu_custom_call" | custom-call | tf_op jit(solution)/shard_map/ffn/pallas_call | solution.py:347
  173.1 1.6 copy.6

commit v2 on v1

v2 whole, which is shorter than its diff:
```python
import functools

import jax
import jax.numpy as jnp
from jax import lax
from jax.experimental import pallas as pl
from jax.experimental.pallas import tpu as pltpu
from jax.sharding import PartitionSpec as P

D = 12288
EPSILON = 1e-05
MESH = pl.DeviceIdType.MESH
F32, BF16 = jnp.float32, jnp.bfloat16

WAVES = 4
LANES = 8
NARROW = 768
BLOCK = 16
TILE = 256
FAR_FIRST = (4, 3, 5, 2, 6, 1, 7)


def gelu(v):
    return 0.5 * v * (1.0 + jnp.tanh(0.7978845608028654 * (v + 0.044715 * (v * v * v))))


def kernel(
    tokens_hbm, gain_hbm, w1_hbm, w2_hbm, out_ref,
    tokens_ref, gain_ref, w1, w2, raw, scaled, part, rs1, rs2, total, active, branch, own, out_send, out_recv, squares, inverse,
    in_sem, w1_sem, w2_sem, tok_ssem, tok_rsem, pair_rsem, out_ssem, out_rsem, sq_ssem, sq_rsem, ring_ssem, ring_rsem,
):
    row, col = lax.axis_index("row"), lax.axis_index("col")
    x, z = lax.rem(row, 4), lax.div(row, 4)

    def w1_copy(s):
        return pltpu.make_async_copy(w1_hbm.at[:, pl.ds(pl.multiple_of(s * NARROW, NARROW), NARROW)], w1.at[s], w1_sem.at[s])

    def w2_copy(s):
        return pltpu.make_async_copy(w2_hbm.at[pl.ds(pl.multiple_of(s * NARROW, NARROW), NARROW)], w2.at[s], w2_sem.at[0])

    inputs = (
        pltpu.make_async_copy(tokens_hbm, tokens_ref, in_sem.at[0]),
        pltpu.make_async_copy(gain_hbm, gain_ref, in_sem.at[1]),
    )
    inputs[0].start()
    barrier = pltpu.get_barrier_semaphore()
    for i in range(1, 8):
        pl.semaphore_signal(barrier, inc=1, device_id=(row, lax.rem(col + i, 8)), device_id_type=MESH)
    for i in range(1, 16):
        pl.semaphore_signal(barrier, inc=1, device_id=(lax.rem(row + i, 16), col), device_id_type=MESH)
    inputs[1].start()
    for s in range(LANES):
        w1_copy(s).start()
    for s in range(LANES):
        w2_copy(s).start()

    inputs[0].wait()
    pl.semaphore_wait(barrier, 22)

    def landed(ref, sem):
        pltpu.make_async_copy(ref, ref, sem).wait()

    partner = col + 1 - 2 * lax.rem(col, 2)

    def tok_copy(w, i):
        return pltpu.make_async_remote_copy(
            src_ref=tokens_ref.at[w], dst_ref=raw.at[col, w], send_sem=tok_ssem.at[0], recv_sem=tok_rsem.at[w],
            device_id=(row, lax.rem(col + 2 * i, 8)), device_id_type=MESH,
        )

    def pair_copy(w, i):
        c = lax.rem(col + 2 * i, 8)
        return pltpu.make_async_remote_copy(
            src_ref=tokens_ref.at[w] if i == 0 else raw.at[c, w], dst_ref=raw.at[c, w],
            send_sem=tok_ssem.at[0], recv_sem=pair_rsem.at[w],
            device_id=(row, partner), device_id_type=MESH,
        )

    for w in range(WAVES):
        for i in (2, 1, 3):
            tok_copy(w, i).start()
        pair_copy(w, 0).start()
    raw[col] = tokens_ref[...]

    def forward_tokens(w):
        landed(raw.at[pl.ds(0, 3), w], tok_rsem.at[w])
        for i in (1, 3, 2):
            pair_copy(w, i).start()

    def wait_tokens(w):
        landed(raw.at[pl.ds(0, 4), w], pair_rsem.at[w])

    def place(s):
        second = lax.rem(s, 2)
        step = 1 - 2 * lax.rem(lax.div(s, 2), 2)
        p = x * (1 - second) + z * second
        q = z * (1 - second) + x * second
        p_next, q_next = lax.rem(p + step + 4, 4), lax.rem(q + step + 4, 4)
        first_row = second * (p_next * 4 + q) + (1 - second) * (q * 4 + p_next)
        second_row = second * (p * 4 + q_next) + (1 - second) * (q_next * 4 + p)
        return p, q, step, first_row, second_row

    def ring_copy(kind, w, s, k, src, dst, target):
        return pltpu.make_async_remote_copy(
            src_ref=src, dst_ref=dst,
            send_sem=ring_ssem.at[kind, s], recv_sem=ring_rsem.at[kind, s, k],
            device_id=(target, col), device_id_type=MESH,
        )

    def around(v):
        return lax.rem(v + 8, 4)

    def rs1_copy(w, s, k, target):
        side = lax.rem(w, 2)
        return ring_copy(0, w, s, k, rs1.at[side, s, (k + 3) % 4], rs1.at[side, s, k], target)

    def rs2_copy(w, s, k, target):
        side = lax.rem(w, 2)
        return ring_copy(1, w, s, k, rs2.at[side, s, (k + 3) % 4], rs2.at[side, s, k], target)

    def ag2_copy(w, s, k, p, q, step, target):
        block = active.at[w, s, p * 4 + around(q - step * k)]
        return ring_copy(2, w, s, k, block, block, target)

    def ag1_copy(w, s, k, p, step, target):
        chunk = active.at[w, s, pl.ds(around(p - step * k) * 4, 4)]
        return ring_copy(3, w, s, k, chunk, chunk, target)

    def own_part(w, s):
        side = lax.rem(w, 2)
        for t in range(NARROW // TILE):
            cols = slice(t * TILE, (t + 1) * TILE)
            got = jnp.dot(scaled[w].reshape(256, 768), w1[s, :, cols], preferred_element_type=F32)
            part[side, s, :, :, cols] = got.reshape(16, BLOCK, TILE)

    def rs1_event(w, s, k):
        p, q, step, target, _ = place(s)
        j = around(p - step * (k + 1))
        side, slot = lax.rem(w, 2), (k + 3) % 4
        mine = part[side, s, pl.ds(j * 4, 4)]
        if k > 0:
            rs1_copy(w, s, k - 1, target).wait_recv()
            mine = mine + rs1[side, s, slot].astype(F32)
        rs1[side, s, slot] = mine.astype(BF16)
        if k > 0:
            rs1_copy(w, s, k - 1, target).wait_send()
        rs1_copy(w, s, k, target).start()

    def rs2_event(w, s, k):
        p, q, step, before, target = place(s)
        j = around(q - step * (k + 1))
        side, slot = lax.rem(w, 2), (k + 3) % 4
        if k == 0:
            rs1_copy(w, s, 2, before).wait_recv()
            total[s] = part[side, s, pl.ds(p * 4, 4)] + rs1[side, s, 2].astype(F32)
            rs1_copy(w, s, 2, before).wait_send()
            rs2[side, s, slot] = total[s, j].astype(BF16)
        else:
            rs2_copy(w, s, k - 1, target).wait_recv()
            rs2[side, s, slot] = (rs2[side, s, slot].astype(F32) + total[s, j]).astype(BF16)
            rs2_copy(w, s, k - 1, target).wait_send()
        rs2_copy(w, s, k, target).start()

    def ag2_event(w, s, k):
        p, q, step, _, target = place(s)
        if k == 0:
            rs2_copy(w, s, 2, target).wait_recv()
            b = p * 4 + q
            c, first = lax.div(b, 2), 32 * w + 16 * lax.rem(b, 2)
            sub = lax.broadcasted_iota(jnp.int32, (8, 128), 0)
            line = jnp.sum(jnp.where(sub == c, inverse[...], 0.0), axis=0, keepdims=True)
            spot = lax.broadcasted_iota(jnp.int32, (BLOCK, 128), 1) == lax.broadcasted_iota(jnp.int32, (BLOCK, 128), 0) + first
            scale = jnp.sum(jnp.where(spot, jnp.broadcast_to(line, (BLOCK, 128)), 0.0), axis=1, keepdims=True)
            hidden = (rs2[lax.rem(w, 2), s, 2].astype(F32) + total[s, q]) * scale
            active[w, s, b] = gelu(hidden).astype(BF16)
            rs2_copy(w, s, 2, target).wait_send()
        else:
            ag2_copy(w, s, k - 1, p, q, step, target).wait_recv()
            ag2_copy(w, s, k - 1, p, q, step, target).wait_send()
        ag2_copy(w, s, k, p, q, step, target).start()

    def ag1_event(w, s, k):
        p, q, step, target, before = place(s)
        if k == 0:
            ag2_copy(w, s, 2, p, q, step, before).wait_recv()
            ag2_copy(w, s, 2, p, q, step, before).wait_send()

            @pl.when(w > 0)
            def _():
                ag1_copy(w, s, 2, p, step, target).wait_send()
        else:
            ag1_copy(w, s, k - 1, p, step, target).wait_recv()
            ag1_copy(w, s, k - 1, p, step, target).wait_send()
        ag1_copy(w, s, k, p, step, target).start()

    def out_copy(w, i):
        peer = lax.rem(col + i, 8)
        return pltpu.make_async_remote_copy(
            src_ref=out_send.at[w, peer], dst_ref=out_recv.at[w, col],
            send_sem=out_ssem.at[0], recv_sem=out_rsem.at[w],
            device_id=(row, peer), device_id_type=MESH,
        )

    def add_chunks(w, s, ks):
        p, q, step, target, _ = place(s)
        side = lax.rem(w, 2)
        if 3 in ks:
            ag1_copy(w, s, 2, p, step, target).wait_recv()
        chunks = [pl.ds(around(p - step * k) * 4, 4) for k in ks]
        a = [active[w, s, chunk].reshape(64, NARROW) for chunk in chunks]
        a = a[0] if len(a) == 1 else jnp.concatenate(a, axis=0)
        for t in range(768 // TILE):
            cols = slice(t * TILE, (t + 1) * TILE)
            got = jnp.dot(a, w2[s, :, cols], preferred_element_type=F32)
            for n, chunk in enumerate(chunks):
                more = got[n * 64:(n + 1) * 64].reshape(4, BLOCK, TILE)
                branch[side, chunk, :, cols] = branch[side, chunk, :, cols] + more

    def send_branch(w):
        side = lax.rem(w, 2)
        out_send[w] = branch[side].reshape(8, 32, 768).astype(BF16)
        own[w] = branch[side, pl.ds(col * 2, 2)].reshape(32, 768)
        for i in FAR_FIRST:
            out_copy(w, i).start()

    def deliver(w):
        rows = own[w] + tokens_ref[w].astype(F32)
        landed(out_recv.at[w, pl.ds(0, 7)], out_rsem.at[w])
        for i in range(1, 8):
            rows = rows + out_recv[w, lax.rem(col + i, 8)].astype(F32)
        out_ref[w] = rows.astype(BF16)

    def sq_copy(i):
        return pltpu.make_async_remote_copy(
            src_ref=squares.at[row], dst_ref=squares.at[row],
            send_sem=sq_ssem.at[0], recv_sem=sq_rsem.at[0],
            device_id=(lax.rem(row + i, 16), col), device_id_type=MESH,
        )

    def square(c):
        v = raw[c].reshape(128, 768).astype(F32)
        v = v * v
        high = v.astype(BF16)
        low = (v - high.astype(F32)).astype(BF16)
        ones, dims = jnp.ones((8, 768), BF16), (((1,), (1,)), ((), ()))
        sums = lax.dot_general(ones, high, dims, preferred_element_type=F32)
        sums = sums + lax.dot_general(ones, low, dims, preferred_element_type=F32)
        squares[row, pl.ds(c, 1)] = sums[:1]

    def take_squares():
        landed(squares.at[pl.ds(0, 15)], sq_rsem.at[0])
        inverse[...] = lax.rsqrt(jnp.sum(squares[...], axis=0) / D + EPSILON)

    def scale_wave(w):
        def one(c, carry):
            v = raw[c, w].astype(F32) * gain_ref[...].reshape(1, 768)
            scaled[w, pl.ds(2 * c, 2)] = v.astype(BF16).reshape(2, BLOCK, NARROW)
            return carry

        lax.fori_loop(0, 8, one, 0)

    inputs[1].wait()
    forward_tokens(0)
    wait_tokens(0)
    scale_wave(0)

    def slot(t, carry):
        for k in range(3):
            if k == 0:
                @pl.when(t == 1)
                def _():
                    wait_tokens(2)
                    wait_tokens(3)

                @pl.when(t == 2)
                def _():
                    take_squares()

                @pl.when(t == 3)
                def _():
                    landed(w2, w2_sem.at[0])

                @pl.when((t >= 3) & (t < 7))
                def _():
                    branch[lax.rem(t + 1, 2)] = jnp.zeros((16, BLOCK, 768), F32)

            if k == 1:
                @pl.when(t == 0)
                def _():
                    forward_tokens(1)

                @pl.when((t >= 1) & (t < 3))
                def _():
                    scale_wave(t + 1)

                @pl.when(t >= 5)
                def _():
                    deliver(t - 5)

            if k == 2:
                @pl.when(t == 0)
                def _():
                    forward_tokens(2)
                    forward_tokens(3)
                    wait_tokens(1)
                    scale_wave(1)

            def lane(s, carry, k=k):
                if k == 0:
                    @pl.when(t == 0)
                    def _():
                        w1_copy(s).wait()
                        own_part(0, s)

                @pl.when((t >= 3) & (t < 7))
                def _():
                    ag1_event(t - 3, s, k)

                @pl.when((t >= 2) & (t < 6))
                def _():
                    ag2_event(t - 2, s, k)

                @pl.when((t >= 1) & (t < 5))
                def _():
                    rs2_event(t - 1, s, k)

                @pl.when(t < 4)
                def _():
                    rs1_event(t, s, k)

                if k == 0:
                    @pl.when(t == 1)
                    def _():
                        square(s)

                    @pl.when(t >= 4)
                    def _():
                        add_chunks(t - 4, s, (2, 3))

                if k == 1:
                    @pl.when((t >= 1) & (t < 3) & (lax.rem(s, 2) == 1))
                    def _():
                        own_part(t + 1, lax.div(s, 2))

                if k == 2:
                    @pl.when((t == 0) | ((t < 3) & (lax.rem(s, 2) == 1)))
                    def _():
                        own_part(t + 1, jnp.where(t == 0, s, 4 + lax.div(s, 2)))

                if k == 1:
                    @pl.when(t >= 3)
                    def _():
                        add_chunks(t - 3, s, (0, 1))

                if k == 2:
                    @pl.when(t == 6)
                    def _():
                        add_chunks(WAVES - 1, s, (2,))

                return carry

            lax.fori_loop(0, LANES, lane, 0)

            if k == 0:
                @pl.when(t == 1)
                def _():
                    for i in range(1, 16):
                        sq_copy(i).start()

                @pl.when(t >= 4)
                def _():
                    send_branch(t - 4)

            if k == 1:
                @pl.when(t == 4)
                def _():
                    landed(raw.at[pl.ds(0, 7)], tok_ssem.at[0])
                    landed(squares.at[pl.ds(0, 15)], sq_ssem.at[0])

            if k == 2:
                @pl.when(t == 6)
                def _():
                    deliver(2)

        return carry

    lax.fori_loop(0, 7, slot, 0)

    def last(s, carry):
        add_chunks(WAVES - 1, s, (3,))
        p, q, step, target, _ = place(s)
        ag1_copy(WAVES - 1, s, 2, p, step, target).wait_send()
        return carry

    lax.fori_loop(0, LANES, last, 0)
    send_branch(WAVES - 1)
    deliver(WAVES - 1)
    landed(out_send.at[:, pl.ds(0, 7)], out_ssem.at[0])


def per_device(tokens, norm_gain, weight_in, weight_out):
    vmem = pl.BlockSpec(memory_space=pltpu.VMEM)
    anywhere = pl.BlockSpec(memory_space=pl.ANY)
    dma = pltpu.SemaphoreType.DMA
    out = pl.pallas_call(
        kernel,
        out_shape=jax.ShapeDtypeStruct((WAVES, 32, NARROW), BF16),
        in_specs=[anywhere] * 4,
        out_specs=vmem,
        scratch_shapes=[
            pltpu.VMEM((WAVES, 32, 768), BF16),
            pltpu.VMEM((768,), F32),
            pltpu.VMEM((LANES, 768, NARROW), BF16),
            pltpu.VMEM((LANES, NARROW, 768), BF16),
            pltpu.VMEM((8, WAVES, 32, 768), BF16),
            pltpu.VMEM((WAVES, 16, BLOCK, 768), BF16),
            pltpu.VMEM((2, LANES, 16, BLOCK, NARROW), F32),
            pltpu.VMEM((2, LANES, 4, 4, BLOCK, NARROW), BF16),
            pltpu.VMEM((2, LANES, 4, BLOCK, NARROW), BF16),
            pltpu.VMEM((LANES, 4, BLOCK, NARROW), F32),
            pltpu.VMEM((WAVES, LANES, 16, BLOCK, NARROW), BF16),
            pltpu.VMEM((2, 16, BLOCK, 768), F32),
            pltpu.VMEM((WAVES, 32, 768), F32),
            pltpu.VMEM((WAVES, 8, 32, 768), BF16),
            pltpu.VMEM((WAVES, 8, 32, 768), BF16),
            pltpu.VMEM((16, 8, 128), F32),
            pltpu.VMEM((8, 128), F32),
            dma((2,)), dma((LANES,)), dma((1,)),
            dma((1,)), dma((WAVES,)), dma((WAVES,)),
            dma((1,)), dma((WAVES,)),
            dma((1,)), dma((1,)),
            dma((4, LANES)), dma((4, LANES, 3)),
        ],
        compiler_params=pltpu.CompilerParams(
            collective_id=0, has_side_effects=True, vmem_limit_bytes=67043328
        ),
        name="ffn",
    )(tokens.reshape(WAVES, 32, 768), norm_gain, weight_in, weight_out)
    return out.reshape(128, 768)


def solution(mesh):
    in_specs = (P("col", "row"), P("row"), P("row", "col"), P("col", "row"))
    out_specs = P("col", "row")
    return jax.shard_map(
        per_device, mesh=mesh, in_specs=in_specs, out_specs=out_specs, check_vma=False
    )
```

time: 175 us -> 157 us (0.90)
  Pallas kernels: 172 us -> 155 us
    pallas_call x1, Pallas kernels: 172 us -> 155 us  [per_device(): pl.pallas_call(kernel, out_shape=jax.ShapeDtypeStruct((WAVES, 32, NARROW)...]
where the time goes in v2:
time: 157 us
  Pallas kernels  155 us (99%)
  local copies, waits for them, and re-layouts  1.62 us (1%)
    pallas_call x1, Pallas kernels, per_device(): pl.pallas_call(kernel, out_shape=jax.ShapeDtypeStruct((WAVES, 32, NARROW)...  155 us

profile of v2, /device:TPU:1, one launch (start us, length us, event | category | flops | bytes accessed | tf_op | source)
XLA Modules:
  0.0 156.9 jit_solution(12626589009396015688)
XLA Ops:
  0.0 155.3 %ffn.1 = bf16[4,32,768]{2,1,0:T(8,128)(2,1)} custom-call(bf16[4,32,768]{2,1,0:T(8,128)(2,1)} %bitcast.3, f32[768]{0:T(1024)} %gain_hbm.1, bf16[768,6144]{1,0:T(8,128)(2,1)} %w1_hbm.1, bf16[6144,768]{1,0:T(8,128)(2,1)} %w2_hbm.1), custom_call_target="tpu_custom_call" | custom-call | tf_op jit(solution)/shard_map/ffn/pallas_call | solution.py:405
  155.3 1.6 %copy.6 = bf16[128,768]{1,0:T(8,128)(2,1)} copy(bf16[128,768]{1,0:T(8,128)(2,1)} %bitcast.2) | data formatting | bytes 393216

commit v3 on v2

--- a/solution.py
+++ b/solution.py
@@ -17,7 +17,6 @@
 NARROW = 768
 BLOCK = 16
 TILE = 256
-FAR_FIRST = (4, 3, 5, 2, 6, 1, 7)
 
 
 def gelu(v):
@@ -51,8 +50,6 @@
     inputs[1].start()
     for s in range(LANES):
         w1_copy(s).start()
-    for s in range(LANES):
-        w2_copy(s).start()
 
     inputs[0].wait()
     pl.semaphore_wait(barrier, 22)
@@ -60,35 +57,50 @@
     def landed(ref, sem):
         pltpu.make_async_copy(ref, ref, sem).wait()
 
-    partner = col + 1 - 2 * lax.rem(col, 2)
-
-    def tok_copy(w, i):
+    y, core = lax.div(col, 2), lax.rem(col, 2)
+    partner = col + 1 - 2 * core
+
+    def beside(n, c):
+        return lax.rem(2 * (y + n) + c, 8)
+
+    def source(w, g):
+        late = lax.div(w, 2)
+        two = lax.div(g, 2)
+        odd = lax.rem(g, 2)
+        early_c, late_c = beside(2 * w, two), beside(1 + 2 * two, odd)
+        return early_c * (1 - late) + late_c * late, 4 * (odd * (1 - late) + (w - 2) * late)
+
+    def tok_copy(w, n):
+        blocks = pl.ds(0, 8) if w == 1 else pl.ds(4 * (w - 2), 4)
         return pltpu.make_async_remote_copy(
-            src_ref=tokens_ref.at[w], dst_ref=raw.at[col, w], send_sem=tok_ssem.at[0], recv_sem=tok_rsem.at[w],
-            device_id=(row, lax.rem(col + 2 * i, 8)), device_id_type=MESH,
+            src_ref=tokens_ref.at[blocks], dst_ref=raw.at[col, blocks],
+            send_sem=tok_ssem.at[0], recv_sem=tok_rsem.at[w],
+            device_id=(row, beside(n, core)), device_id_type=MESH,
         )
 
-    def pair_copy(w, i):
-        c = lax.rem(col + 2 * i, 8)
+    def pair_copy(w, n):
+        c = beside(n, core)
+        blocks = pl.ds(0, 8) if w < 2 else pl.ds(4 * (w - 2), 4)
         return pltpu.make_async_remote_copy(
-            src_ref=tokens_ref.at[w] if i == 0 else raw.at[c, w], dst_ref=raw.at[c, w],
+            src_ref=tokens_ref.at[blocks] if w == 0 else raw.at[c, blocks], dst_ref=raw.at[c, blocks],
             send_sem=tok_ssem.at[0], recv_sem=pair_rsem.at[w],
             device_id=(row, partner), device_id_type=MESH,
         )
 
-    for w in range(WAVES):
-        for i in (2, 1, 3):
-            tok_copy(w, i).start()
-        pair_copy(w, 0).start()
+    pair_copy(0, 0).start()
+    tok_copy(1, 2).start()
+    for w in (2, 3):
+        for n in (1, 3):
+            tok_copy(w, n).start()
     raw[col] = tokens_ref[...]
 
     def forward_tokens(w):
-        landed(raw.at[pl.ds(0, 3), w], tok_rsem.at[w])
-        for i in (1, 3, 2):
-            pair_copy(w, i).start()
+        landed(raw.at[0], tok_rsem.at[w])
+        for n in (2,) if w == 1 else (1, 3):
+            pair_copy(w, n).start()
 
     def wait_tokens(w):
-        landed(raw.at[pl.ds(0, 4), w], pair_rsem.at[w])
+        landed(raw.at[0], pair_rsem.at[w])
 
     def place(s):
         second = lax.rem(s, 2)
@@ -103,7 +115,7 @@
     def ring_copy(kind, w, s, k, src, dst, target):
         return pltpu.make_async_remote_copy(
             src_ref=src, dst_ref=dst,
-            send_sem=ring_ssem.at[kind, s], recv_sem=ring_rsem.at[kind, s, k],
+            send_sem=ring_ssem.at[kind, s], recv_sem=ring_rsem.at[kind if kind < 3 else 3 + lax.rem(w, 2), s, k],
             device_id=(target, col), device_id_type=MESH,
         )
 
@@ -166,7 +178,8 @@
         if k == 0:
             rs2_copy(w, s, 2, target).wait_recv()
             b = p * 4 + q
-            c, first = lax.div(b, 2), 32 * w + 16 * lax.rem(b, 2)
+            c, at = source(w, lax.div(b, 4))
+            first = 16 * (at + lax.rem(b, 4))
             sub = lax.broadcasted_iota(jnp.int32, (8, 128), 0)
             line = jnp.sum(jnp.where(sub == c, inverse[...], 0.0), axis=0, keepdims=True)
             spot = lax.broadcasted_iota(jnp.int32, (BLOCK, 128), 1) == lax.broadcasted_iota(jnp.int32, (BLOCK, 128), 0) + first
@@ -193,12 +206,12 @@
             ag1_copy(w, s, k - 1, p, step, target).wait_send()
         ag1_copy(w, s, k, p, step, target).start()
 
-    def out_copy(w, i):
-        peer = lax.rem(col + i, 8)
+    def out_copy(w, g, blocks):
+        c, at = source(w, g)
         return pltpu.make_async_remote_copy(
-            src_ref=out_send.at[w, peer], dst_ref=out_recv.at[w, col],
+            src_ref=out_send.at[w, pl.ds(4 * g, blocks)], dst_ref=out_recv.at[col, pl.ds(at, blocks)],
             send_sem=out_ssem.at[0], recv_sem=out_rsem.at[w],
-            device_id=(row, peer), device_id_type=MESH,
+            device_id=(row, c), device_id_type=MESH,
         )
 
     def add_chunks(w, s, ks):
@@ -218,17 +231,35 @@
 
     def send_branch(w):
         side = lax.rem(w, 2)
-        out_send[w] = branch[side].reshape(8, 32, 768).astype(BF16)
-        own[w] = branch[side, pl.ds(col * 2, 2)].reshape(32, 768)
-        for i in FAR_FIRST:
-            out_copy(w, i).start()
-
-    def deliver(w):
-        rows = own[w] + tokens_ref[w].astype(F32)
-        landed(out_recv.at[w, pl.ds(0, 7)], out_rsem.at[w])
-        for i in range(1, 8):
-            rows = rows + out_recv[w, lax.rem(col + i, 8)].astype(F32)
-        out_ref[w] = rows.astype(BF16)
+
+        @pl.when(w == 0)
+        def _():
+            g = 2 - 2 * core
+            out_send[0, pl.ds(4 * g, 8)] = branch[side, pl.ds(4 * g, 8)].astype(BF16)
+            out_copy(0, g, 8).start()
+            own[...] = branch[side, pl.ds(8 * core, 8)]
+
+        @pl.when(w == 1)
+        def _():
+            for g in (0, 2):
+                out_send[1, pl.ds(4 * g, 8)] = branch[side, pl.ds(4 * g, 8)].astype(BF16)
+                out_copy(1, g, 8).start()
+
+        @pl.when(w > 1)
+        def _():
+            for g in (0, 2, 1, 3):
+                out_send[w, pl.ds(4 * g, 4)] = branch[side, pl.ds(4 * g, 4)].astype(BF16)
+                out_copy(w, g, 4).start()
+
+    def deliver(h):
+        blocks = pl.ds(4 * h, 4)
+        rows = own[blocks] + tokens_ref[blocks].astype(F32)
+        for n, c in ((0, 1 - core), (2, 0), (2, 1)):
+            rows = rows + out_recv[beside(n, c), blocks].astype(F32)
+        landed(out_recv.at[pl.ds(0, 2)], out_rsem.at[2 + h])
+        for n, c in ((1, 0), (1, 1), (3, 0), (3, 1)):
+            rows = rows + out_recv[beside(n, c), blocks].astype(F32)
+        out_ref[blocks] = rows.astype(BF16)
 
     def sq_copy(i):
         return pltpu.make_async_remote_copy(
@@ -252,15 +283,15 @@
         inverse[...] = lax.rsqrt(jnp.sum(squares[...], axis=0) / D + EPSILON)
 
     def scale_wave(w):
-        def one(c, carry):
-            v = raw[c, w].astype(F32) * gain_ref[...].reshape(1, 768)
-            scaled[w, pl.ds(2 * c, 2)] = v.astype(BF16).reshape(2, BLOCK, NARROW)
+        def one(g, carry):
+            c, at = source(w, g)
+            v = raw[c, pl.ds(at, 4)].reshape(64, 768).astype(F32) * gain_ref[...].reshape(1, 768)
+            scaled[w, pl.ds(4 * g, 4)] = v.astype(BF16).reshape(4, BLOCK, 768)
             return carry
 
-        lax.fori_loop(0, 8, one, 0)
+        lax.fori_loop(0, 4, one, 0)
 
     inputs[1].wait()
-    forward_tokens(0)
     wait_tokens(0)
     scale_wave(0)
 
@@ -269,8 +300,8 @@
             if k == 0:
                 @pl.when(t == 1)
                 def _():
-                    wait_tokens(2)
-                    wait_tokens(3)
+                    forward_tokens(2)
+                    forward_tokens(3)
 
                 @pl.when(t == 2)
                 def _():
@@ -285,25 +316,14 @@
                     branch[lax.rem(t + 1, 2)] = jnp.zeros((16, BLOCK, 768), F32)
 
             if k == 1:
-                @pl.when(t == 0)
-                def _():
-                    forward_tokens(1)
-
-                @pl.when((t >= 1) & (t < 3))
+                @pl.when((t > 0) & (t < 3))
                 def _():
                     scale_wave(t + 1)
-
-                @pl.when(t >= 5)
-                def _():
-                    deliver(t - 5)
 
             if k == 2:
                 @pl.when(t == 0)
                 def _():
-                    forward_tokens(2)
-                    forward_tokens(3)
-                    wait_tokens(1)
-                    scale_wave(1)
+                    forward_tokens(1)
 
             def lane(s, carry, k=k):
                 if k == 0:
@@ -312,6 +332,10 @@
                         w1_copy(s).wait()
                         own_part(0, s)
 
+                    @pl.when((t == 1) & (s >= 4))
+                    def _():
+                        own_part(1, s)
+
                 @pl.when((t >= 3) & (t < 7))
                 def _():
                     ag1_event(t - 3, s, k)
@@ -329,73 +353,83 @@
                     rs1_event(t, s, k)
 
                 if k == 0:
+                    @pl.when((t == 1) & (s == 4))
+                    def _():
+                        wait_tokens(2)
+                        wait_tokens(3)
+
                     @pl.when(t == 1)
                     def _():
-                        square(s)
-
+                        near = lax.div(s, 4)
+                        square((1 - near) * beside(2 * lax.div(s, 2), lax.rem(s, 2)) + near * beside(1 + 2 * lax.div(s - 4 * near, 2), lax.rem(s, 2)))
+
+                if k > 0:
+                    @pl.when((t > 0) & (t < 3) & (lax.rem(s, 2) == 1))
+                    def _():
+                        own_part(t + 1, 4 * (k - 1) + lax.div(s, 2))
+
+                if k == 2:
+                    @pl.when((t == 0) & (s == 3))
+                    def _():
+                        wait_tokens(1)
+                        scale_wave(1)
+
+                    @pl.when((t == 0) & (s >= 4))
+                    def _():
+                        own_part(1, s - 4)
+
+                if k == 1:
                     @pl.when(t >= 4)
                     def _():
                         add_chunks(t - 4, s, (2, 3))
 
-                if k == 1:
-                    @pl.when((t >= 1) & (t < 3) & (lax.rem(s, 2) == 1))
-                    def _():
-                        own_part(t + 1, lax.div(s, 2))
-
                 if k == 2:
-                    @pl.when((t == 0) | ((t < 3) & (lax.rem(s, 2) == 1)))
-                    def _():
-                        own_part(t + 1, jnp.where(t == 0, s, 4 + lax.div(s, 2)))
-
-                if k == 1:
                     @pl.when(t >= 3)
                     def _():
                         add_chunks(t - 3, s, (0, 1))
 
-                if k == 2:
-                    @pl.when(t == 6)
-                    def _():
-                        add_chunks(WAVES - 1, s, (2,))
-
                 return carry
 
             lax.fori_loop(0, LANES, lane, 0)
 
             if k == 0:
+                @pl.when(t == 0)
+                def _():
+                    for s in range(LANES):
+                        w2_copy(s).start()
+
                 @pl.when(t == 1)
                 def _():
                     for i in range(1, 16):
                         sq_copy(i).start()
 
+            if k == 1:
                 @pl.when(t >= 4)
                 def _():
                     send_branch(t - 4)
 
-            if k == 1:
                 @pl.when(t == 4)
                 def _():
                     landed(raw.at[pl.ds(0, 7)], tok_ssem.at[0])
                     landed(squares.at[pl.ds(0, 15)], sq_ssem.at[0])
 
-            if k == 2:
-                @pl.when(t == 6)
-                def _():
-                    deliver(2)
-
         return carry
 
     lax.fori_loop(0, 7, slot, 0)
 
     def last(s, carry):
-        add_chunks(WAVES - 1, s, (3,))
+        add_chunks(WAVES - 1, s, (2, 3))
         p, q, step, target, _ = place(s)
         ag1_copy(WAVES - 1, s, 2, p, step, target).wait_send()
         return carry
 
     lax.fori_loop(0, LANES, last, 0)
     send_branch(WAVES - 1)
-    deliver(WAVES - 1)
-    landed(out_send.at[:, pl.ds(0, 7)], out_ssem.at[0])
+    landed(out_recv.at[0], out_rsem.at[0])
+    landed(out_recv.at[pl.ds(0, 2)], out_rsem.at[1])
+    deliver(0)
+    deliver(1)
+    landed(out_send.at[:, pl.ds(0, 14)], out_ssem.at[0])
 
 
 def per_device(tokens, norm_gain, weight_in, weight_out):
@@ -404,15 +438,15 @@
     dma = pltpu.SemaphoreType.DMA
     out = pl.pallas_call(
         kernel,
-        out_shape=jax.ShapeDtypeStruct((WAVES, 32, NARROW), BF16),
+        out_shape=jax.ShapeDtypeStruct((8, BLOCK, 768), BF16),
         in_specs=[anywhere] * 4,
         out_specs=vmem,
         scratch_shapes=[
-            pltpu.VMEM((WAVES, 32, 768), BF16),
+            pltpu.VMEM((8, BLOCK, 768), BF16),
             pltpu.VMEM((768,), F32),
             pltpu.VMEM((LANES, 768, NARROW), BF16),
             pltpu.VMEM((LANES, NARROW, 768), BF16),
-            pltpu.VMEM((8, WAVES, 32, 768), BF16),
+            pltpu.VMEM((8, 8, BLOCK, 768), BF16),
             pltpu.VMEM((WAVES, 16, BLOCK, 768), BF16),
             pltpu.VMEM((2, LANES, 16, BLOCK, NARROW), F32),
             pltpu.VMEM((2, LANES, 4, 4, BLOCK, NARROW), BF16),
@@ -420,22 +454,22 @@
             pltpu.VMEM((LANES, 4, BLOCK, NARROW), F32),
             pltpu.VMEM((WAVES, LANES, 16, BLOCK, NARROW), BF16),
             pltpu.VMEM((2, 16, BLOCK, 768), F32),
-            pltpu.VMEM((WAVES, 32, 768), F32),
-            pltpu.VMEM((WAVES, 8, 32, 768), BF16),
-            pltpu.VMEM((WAVES, 8, 32, 768), BF16),
+            pltpu.VMEM((8, BLOCK, 768), F32),
+            pltpu.VMEM((WAVES, 16, BLOCK, 768), BF16),
+            pltpu.VMEM((8, 8, BLOCK, 768), BF16),
             pltpu.VMEM((16, 8, 128), F32),
             pltpu.VMEM((8, 128), F32),
             dma((2,)), dma((LANES,)), dma((1,)),
             dma((1,)), dma((WAVES,)), dma((WAVES,)),
             dma((1,)), dma((WAVES,)),
             dma((1,)), dma((1,)),
-            dma((4, LANES)), dma((4, LANES, 3)),
+            dma((4, LANES)), dma((5, LANES, 3)),
         ],
         compiler_params=pltpu.CompilerParams(
             collective_id=0, has_side_effects=True, vmem_limit_bytes=67043328
         ),
         name="ffn",
-    )(tokens.reshape(WAVES, 32, 768), norm_gain, weight_in, weight_out)
+    )(tokens.reshape(8, BLOCK, 768), norm_gain, weight_in, weight_out)
     return out.reshape(128, 768)
 
 

time: 157 us -> 153 us (0.975)
  Pallas kernels: 155 us -> 152 us
    pallas_call x1, Pallas kernels: 155 us -> 152 us  [per_device(): pl.pallas_call(kernel, out_shape=jax.ShapeDtypeStruct((8, BLOCK, 768), BF...]
where the time goes in v3:
time: 153 us
  Pallas kernels  152 us (99%)
  local copies, waits for them, and re-layouts  1.62 us (1%)
    pallas_call x1, Pallas kernels, per_device(): pl.pallas_call(kernel, out_shape=jax.ShapeDtypeStruct((8, BLOCK, 768), BF...  152 us

profile of v3, /device:TPU:1, one launch (start us, length us, event | category | flops | bytes accessed | tf_op | source)
XLA Modules:
  0.0 153.1 jit_solution(17112414963916253051)
XLA Ops:
  0.0 151.5 %ffn.1 = bf16[8,16,768]{2,1,0:T(8,128)(2,1)} custom-call(bf16[8,16,768]{2,1,0:T(8,128)(2,1)} %bitcast.3, f32[768]{0:T(1024)} %gain_hbm.1, bf16[768,6144]{1,0:T(8,128)(2,1)} %w1_hbm.1, bf16[6144,768]{1,0:T(8,128)(2,1)} %w2_hbm.1), custom_call_target="tpu_custom_call" | custom-call | tf_op jit(solution)/shard_map/ffn/pallas_call | solution.py:439
  151.5 1.6 %copy.6 = bf16[128,768]{1,0:T(8,128)(2,1)} copy(bf16[128,768]{1,0:T(8,128)(2,1)} %bitcast.2) | data formatting | bytes 393216

commit v4 on v3

--- a/solution.py
+++ b/solution.py
@@ -45,14 +45,15 @@
     barrier = pltpu.get_barrier_semaphore()
     for i in range(1, 8):
         pl.semaphore_signal(barrier, inc=1, device_id=(row, lax.rem(col + i, 8)), device_id_type=MESH)
-    for i in range(1, 16):
-        pl.semaphore_signal(barrier, inc=1, device_id=(lax.rem(row + i, 16), col), device_id_type=MESH)
+    for i in range(1, 4):
+        pl.semaphore_signal(barrier, inc=1, device_id=(4 * z + lax.rem(x + i, 4), col), device_id_type=MESH)
+        pl.semaphore_signal(barrier, inc=1, device_id=(4 * lax.rem(z + i, 4) + x, col), device_id_type=MESH)
     inputs[1].start()
-    for s in range(LANES):
+    for s in range(4):
         w1_copy(s).start()
 
     inputs[0].wait()
-    pl.semaphore_wait(barrier, 22)
+    pl.semaphore_wait(barrier, 13)
 
     def landed(ref, sem):
         pltpu.make_async_copy(ref, ref, sem).wait()
@@ -88,10 +89,6 @@
         )
 
     pair_copy(0, 0).start()
-    tok_copy(1, 2).start()
-    for w in (2, 3):
-        for n in (1, 3):
-            tok_copy(w, n).start()
     raw[col] = tokens_ref[...]
 
     def forward_tokens(w):
@@ -115,7 +112,7 @@
     def ring_copy(kind, w, s, k, src, dst, target):
         return pltpu.make_async_remote_copy(
             src_ref=src, dst_ref=dst,
-            send_sem=ring_ssem.at[kind, s], recv_sem=ring_rsem.at[kind if kind < 3 else 3 + lax.rem(w, 2), s, k],
+            send_sem=ring_ssem.at[kind, s], recv_sem=ring_rsem.at[kind, s, k],
             device_id=(target, col), device_id_type=MESH,
         )
 
@@ -217,8 +214,6 @@
     def add_chunks(w, s, ks):
         p, q, step, target, _ = place(s)
         side = lax.rem(w, 2)
-        if 3 in ks:
-            ag1_copy(w, s, 2, p, step, target).wait_recv()
         chunks = [pl.ds(around(p - step * k) * 4, 4) for k in ks]
         a = [active[w, s, chunk].reshape(64, NARROW) for chunk in chunks]
         a = a[0] if len(a) == 1 else jnp.concatenate(a, axis=0)
@@ -261,11 +256,13 @@
             rows = rows + out_recv[beside(n, c), blocks].astype(F32)
         out_ref[blocks] = rows.astype(BF16)
 
-    def sq_copy(i):
+    def sq_copy(stage, i):
+        place_here = z if stage else x
+        peer = 4 * lax.rem(z + i, 4) + x if stage else 4 * z + lax.rem(x + i, 4)
         return pltpu.make_async_remote_copy(
-            src_ref=squares.at[row], dst_ref=squares.at[row],
-            send_sem=sq_ssem.at[0], recv_sem=sq_rsem.at[0],
-            device_id=(lax.rem(row + i, 16), col), device_id_type=MESH,
+            src_ref=squares.at[stage, place_here], dst_ref=squares.at[stage, place_here],
+            send_sem=sq_ssem.at[0], recv_sem=sq_rsem.at[stage],
+            device_id=(peer, col), device_id_type=MESH,
         )
 
     def square(c):
@@ -276,11 +273,17 @@
         ones, dims = jnp.ones((8, 768), BF16), (((1,), (1,)), ((), ()))
         sums = lax.dot_general(ones, high, dims, preferred_element_type=F32)
         sums = sums + lax.dot_general(ones, low, dims, preferred_element_type=F32)
-        squares[row, pl.ds(c, 1)] = sums[:1]
+        squares[0, x, pl.ds(c, 1)] = sums[:1]
+
+    def pass_squares():
+        landed(squares.at[0, pl.ds(0, 3)], sq_rsem.at[0])
+        squares[1, z] = jnp.sum(squares[0], axis=0)
+        for i in range(1, 4):
+            sq_copy(1, i).start()
 
     def take_squares():
-        landed(squares.at[pl.ds(0, 15)], sq_rsem.at[0])
-        inverse[...] = lax.rsqrt(jnp.sum(squares[...], axis=0) / D + EPSILON)
+        landed(squares.at[0, pl.ds(0, 3)], sq_rsem.at[1])
+        inverse[...] = lax.rsqrt(jnp.sum(squares[1], axis=0) / D + EPSILON)
 
     def scale_wave(w):
         def one(g, carry):
@@ -293,7 +296,13 @@
 
     inputs[1].wait()
     wait_tokens(0)
+    tok_copy(1, 2).start()
+    for w in (2, 3):
+        for n in (1, 3):
+            tok_copy(w, n).start()
     scale_wave(0)
+    for s in range(4, LANES):
+        w1_copy(s).start()
 
     def slot(t, carry):
         for k in range(3):
@@ -363,6 +372,11 @@
                         near = lax.div(s, 4)
                         square((1 - near) * beside(2 * lax.div(s, 2), lax.rem(s, 2)) + near * beside(1 + 2 * lax.div(s - 4 * near, 2), lax.rem(s, 2)))
 
+                    @pl.when(t >= 4)
+                    def _():
+                        p, q, step, target, _ = place(s)
+                        ag1_copy(t - 4, s, 2, p, step, target).wait_recv()
+
                 if k > 0:
                     @pl.when((t > 0) & (t < 3) & (lax.rem(s, 2) == 1))
                     def _():
@@ -400,10 +414,14 @@
 
                 @pl.when(t == 1)
                 def _():
-                    for i in range(1, 16):
-                        sq_copy(i).start()
+                    for i in range(1, 4):
+                        sq_copy(0, i).start()
 
             if k == 1:
+                @pl.when(t == 1)
+                def _():
+                    pass_squares()
+
                 @pl.when(t >= 4)
                 def _():
                     send_branch(t - 4)
@@ -411,15 +429,16 @@
                 @pl.when(t == 4)
                 def _():
                     landed(raw.at[pl.ds(0, 7)], tok_ssem.at[0])
-                    landed(squares.at[pl.ds(0, 15)], sq_ssem.at[0])
+                    landed(squares.at[:, pl.ds(0, 3)], sq_ssem.at[0])
 
         return carry
 
     lax.fori_loop(0, 7, slot, 0)
 
     def last(s, carry):
+        p, q, step, target, _ = place(s)
+        ag1_copy(WAVES - 1, s, 2, p, step, target).wait_recv()
         add_chunks(WAVES - 1, s, (2, 3))
-        p, q, step, target, _ = place(s)
         ag1_copy(WAVES - 1, s, 2, p, step, target).wait_send()
         return carry
 
@@ -457,13 +476,13 @@
             pltpu.VMEM((8, BLOCK, 768), F32),
             pltpu.VMEM((WAVES, 16, BLOCK, 768), BF16),
             pltpu.VMEM((8, 8, BLOCK, 768), BF16),
-            pltpu.VMEM((16, 8, 128), F32),
+            pltpu.VMEM((2, 4, 8, 128), F32),
             pltpu.VMEM((8, 128), F32),
             dma((2,)), dma((LANES,)), dma((1,)),
             dma((1,)), dma((WAVES,)), dma((WAVES,)),
             dma((1,)), dma((WAVES,)),
-            dma((1,)), dma((1,)),
-            dma((4, LANES)), dma((5, LANES, 3)),
+            dma((1,)), dma((2,)),
+            dma((4, LANES)), dma((4, LANES, 3)),
         ],
         compiler_params=pltpu.CompilerParams(
             collective_id=0, has_side_effects=True, vmem_limit_bytes=67043328

time: 153 us -> 151 us (0.987)
  Pallas kernels: 152 us -> 150 us
    pallas_call x1, Pallas kernels: 152 us -> 150 us  [per_device(): pl.pallas_call(kernel, out_shape=jax.ShapeDtypeStruct((8, BLOCK, 768), BF...]
where the time goes in v4:
time: 151 us
  Pallas kernels  150 us (99%)
  local copies, waits for them, and re-layouts  1.62 us (1%)
    pallas_call x1, Pallas kernels, per_device(): pl.pallas_call(kernel, out_shape=jax.ShapeDtypeStruct((8, BLOCK, 768), BF...  150 us

profile of v4, /device:TPU:1, one launch (start us, length us, event | category | flops | bytes accessed | tf_op | source)
XLA Modules:
  0.0 151.2 jit_solution(10160615958194638638)
XLA Ops:
  0.0 149.5 %ffn.1 = bf16[8,16,768]{2,1,0:T(8,128)(2,1)} custom-call(bf16[8,16,768]{2,1,0:T(8,128)(2,1)} %bitcast.3, f32[768]{0:T(1024)} %gain_hbm.1, bf16[768,6144]{1,0:T(8,128)(2,1)} %w1_hbm.1, bf16[6144,768]{1,0:T(8,128)(2,1)} %w2_hbm.1), custom_call_target="tpu_custom_call" | custom-call | tf_op jit(solution)/shard_map/ffn/pallas_call | solution.py:458
  149.6 1.6 %copy.6 = bf16[128,768]{1,0:T(8,128)(2,1)} copy(bf16[128,768]{1,0:T(8,128)(2,1)} %bitcast.2) | data formatting | bytes 393216

commit v5 on v4

--- a/solution.py
+++ b/solution.py
@@ -304,6 +304,9 @@
     for s in range(4, LANES):
         w1_copy(s).start()
 
+    def in_turn(s):
+        return s + (1 - core) * (2 - 4 * lax.rem(lax.div(s, 2), 2))
+
     def slot(t, carry):
         for k in range(3):
             if k == 0:
@@ -335,31 +338,32 @@
                     forward_tokens(1)
 
             def lane(s, carry, k=k):
+                e = in_turn(s)
                 if k == 0:
                     @pl.when(t == 0)
                     def _():
-                        w1_copy(s).wait()
-                        own_part(0, s)
+                        w1_copy(e).wait()
+                        own_part(0, e)
 
                     @pl.when((t == 1) & (s >= 4))
                     def _():
-                        own_part(1, s)
+                        own_part(1, e)
 
                 @pl.when((t >= 3) & (t < 7))
                 def _():
-                    ag1_event(t - 3, s, k)
+                    ag1_event(t - 3, e, k)
 
                 @pl.when((t >= 2) & (t < 6))
                 def _():
-                    ag2_event(t - 2, s, k)
+                    ag2_event(t - 2, e, k)
 
                 @pl.when((t >= 1) & (t < 5))
                 def _():
-                    rs2_event(t - 1, s, k)
+                    rs2_event(t - 1, e, k)
 
                 @pl.when(t < 4)
                 def _():
-                    rs1_event(t, s, k)
+                    rs1_event(t, e, k)
 
                 if k == 0:
                     @pl.when((t == 1) & (s == 4))
@@ -374,8 +378,8 @@
 
                     @pl.when(t >= 4)
                     def _():
-                        p, q, step, target, _ = place(s)
-                        ag1_copy(t - 4, s, 2, p, step, target).wait_recv()
+                        p, q, step, target, _ = place(e)
+                        ag1_copy(t - 4, e, 2, p, step, target).wait_recv()
 
                 if k > 0:
                     @pl.when((t > 0) & (t < 3) & (lax.rem(s, 2) == 1))
@@ -395,12 +399,12 @@
                 if k == 1:
                     @pl.when(t >= 4)
                     def _():
-                        add_chunks(t - 4, s, (2, 3))
+                        add_chunks(t - 4, e, (2, 3))
 
                 if k == 2:
                     @pl.when(t >= 3)
                     def _():
-                        add_chunks(t - 3, s, (0, 1))
+                        add_chunks(t - 3, e, (0, 1))
 
                 return carry
 
@@ -436,6 +440,7 @@
     lax.fori_loop(0, 7, slot, 0)
 
     def last(s, carry):
+        s = in_turn(s)
         p, q, step, target, _ = place(s)
         ag1_copy(WAVES - 1, s, 2, p, step, target).wait_recv()
         add_chunks(WAVES - 1, s, (2, 3))

time: 151 us -> 151 us (level)
  no operation moved by 1% of the time
where the time goes in v5:
time: 151 us
  Pallas kernels  149 us (99%)
  local copies, waits for them, and re-layouts  1.62 us (1%)
    pallas_call x1, Pallas kernels, per_device(): pl.pallas_call(kernel, out_shape=jax.ShapeDtypeStruct((8, BLOCK, 768), BF...  149 us

profile of v5, /device:TPU:1, one launch (start us, length us, event | category | flops | bytes accessed | tf_op | source)
XLA Modules:
  0.0 150.8 jit_solution(16576407828123075774)
XLA Ops:
  0.0 149.2 %ffn.1 = bf16[8,16,768]{2,1,0:T(8,128)(2,1)} custom-call(bf16[8,16,768]{2,1,0:T(8,128)(2,1)} %bitcast.3, f32[768]{0:T(1024)} %gain_hbm.1, bf16[768,6144]{1,0:T(8,128)(2,1)} %w1_hbm.1, bf16[6144,768]{1,0:T(8,128)(2,1)} %w2_hbm.1), custom_call_target="tpu_custom_call" | custom-call | tf_op jit(solution)/shard_map/ffn/pallas_call | solution.py:463
  149.2 1.6 %copy.6 = bf16[128,768]{1,0:T(8,128)(2,1)} copy(bf16[128,768]{1,0:T(8,128)(2,1)} %bitcast.2) | data formatting | bytes 393216
